TPU v7x, 32 devices: a whole 2x2x4 slice. The times are simulated.
32 devices in a mesh: seq: 16 (over z, y, core), grp: 2 (over x).
Axes of the slice: x: 2, y: 2, z: 4, core: 2. Of those that a mesh axis runs over, the one named last changes fastest.
Arguments:
- queries: bfloat16 [4096, 3584], P(('grp', 'seq')), parts along dimension 0, may hold values from -5 to 5
- keys: bfloat16 [4096, 512], P(('grp', 'seq')), parts along dimension 0, may hold values from -5 to 5
- values: bfloat16 [4096, 512], P(('grp', 'seq')), parts along dimension 0, may hold values from -6 to 6
- doc_lengths: int32 [16], P('grp'), parts along dimension 0, may hold values from 1 to 1280, 2048 in all
Outputs:
- attended: bfloat16 [4096, 3584], P(('grp', 'seq')), parts along dimension 0
There are 2 independent parts, one for each index of `grp`. A program takes and returns all parts, laid end to end along the dimension named above; each array names one. Nothing has to cross between parts.
Inputs may be any that keep to these rules, and one draw needn't show every extreme that they name: `doc_lengths`: the 8 documents lie one after another and their lengths sum to 2048; the longest has exactly 1280 tokens.
All inputs are finite; a program needn't handle non-finite values.
Results may differ from a plain program's by a relative error of at most 0.0085.
Values may be sent and summed in bfloat16 or wider, within the bound.
A program may use at most 192 MiB of HBM per device.

v0:
```python
import jax
import jax.numpy as jnp
from jax import lax
from jax.sharding import PartitionSpec as P

HEADS = 28
KV_HEADS = 4
HEAD_DIM = 128


rope_base = 1000000.0
negative = -1e30


def doc_place(position, doc_lengths):
    doc_ends = jnp.cumsum(doc_lengths)
    beyond = position[:, None] >= doc_ends[None, :]
    doc_index = jnp.sum(beyond.astype(jnp.int32), axis=1)
    doc_start = jnp.sum(jnp.where(beyond, doc_lengths[None, :], 0), axis=1)
    return (doc_index, doc_start)


def rotate(values_in, within_doc, head_count):
    row_count = values_in.shape[0]
    half_dim = HEAD_DIM // 2
    inverse_freq = jnp.power(
        jnp.float32(rope_base), -2.0 * jnp.arange(half_dim, dtype=jnp.float32) / HEAD_DIM
    )
    angles = within_doc.astype(jnp.float32)[:, None] * inverse_freq[None, :]
    cosine = jnp.cos(angles)[:, None, :]
    sines = jnp.sin(angles)[:, None, :]
    fields = values_in.astype(jnp.float32).reshape(row_count, head_count, HEAD_DIM)
    lower_half = fields[..., :half_dim]
    upper_half = fields[..., half_dim:]
    rotated = jnp.concatenate(
        [lower_half * cosine - upper_half * sines, upper_half * cosine + lower_half * sines],
        axis=-1,
    )
    return rotated.reshape(row_count, head_count * HEAD_DIM).astype(jnp.bfloat16)


def per_device(queries, keys, values, doc_lengths):
    row_count = queries.shape[0]
    dev_index = lax.axis_index("seq")
    group_size = HEADS // KV_HEADS
    score_scale = HEAD_DIM ** (-0.5)
    local_rows = jnp.arange(row_count, dtype=jnp.int32)
    own_pos = dev_index * row_count + local_rows
    own_start = doc_place(own_pos, doc_lengths)[1]
    within_doc = own_pos - own_start
    q_rot = rotate(queries, within_doc, HEADS)
    k_rot = rotate(keys, within_doc, KV_HEADS)
    query_doc = doc_place(own_pos, doc_lengths)[0]
    q_heads = q_rot.reshape(row_count, KV_HEADS, group_size, HEAD_DIM)
    k_piece = lax.all_gather(k_rot, "seq", axis=0, tiled=True)
    v_piece = lax.all_gather(values, "seq", axis=0, tiled=True)
    length = k_piece.shape[0]
    key_pos = jnp.arange(length, dtype=jnp.int32)
    key_doc = doc_place(key_pos, doc_lengths)[0]
    allowed = (key_doc[None, :] == query_doc[:, None]) & (key_pos[None, :] <= own_pos[:, None])
    allowed_wide = allowed[:, None, None, :]
    running_max = jnp.full((row_count, KV_HEADS, group_size), negative, jnp.float32)
    k_heads = k_piece.reshape(length, KV_HEADS, HEAD_DIM)
    v_heads = v_piece.reshape(length, KV_HEADS, HEAD_DIM)
    scores = (
        jnp.einsum("qkgd,skd->qkgs", q_heads, k_heads, preferred_element_type=jnp.float32)
        * score_scale
    )
    scores = jnp.where(allowed_wide, scores, negative)
    new_max = jnp.maximum(running_max, jnp.max(scores, axis=-1))
    weight = jnp.where(allowed_wide, jnp.exp(scores - new_max[..., None]), 0.0)
    weight_sum = jnp.sum(weight, axis=-1)
    weighted = jnp.einsum(
        "qkgs,skd->qkgd", weight.astype(jnp.bfloat16), v_heads, preferred_element_type=jnp.float32
    )
    running_max, weight_sum, weighted = (new_max, weight_sum, weighted)
    attended = (
        (weighted / weight_sum[..., None]).reshape(row_count, HEADS * HEAD_DIM).astype(jnp.bfloat16)
    )
    return attended


def solution(mesh):
    return jax.shard_map(
        per_device,
        mesh=mesh,
        in_specs=(
            P(("grp", "seq"), None),
            P(("grp", "seq"), None),
            P(("grp", "seq"), None),
            P("grp"),
        ),
        out_specs=P(("grp", "seq"), None),
        check_vma=False,
    )
```

profile of v0, /device:TPU:0, one launch (start us, length us, event | category | flops | bytes accessed | tf_op | source)
XLA Modules:
  0.0 121.0 jit_solution(10799247144488770682)
XLA Ops:
  6.5 0.0 all-gather.3.cloned.1.call-start
  6.6 0.8 reduce-window.8
  7.4 0.7 fusion.10
  8.2 1.0 copy.31
  9.2 0.2 multiply_cosine_fusion
  9.4 0.7 pad_maximum_fusion.1
  10.1 0.0 all-gather.3.cloned.1.call-update
  10.1 0.0 all-gather.5.cloned.1.call-start
  10.1 0.7 all-gather.5.cloned.1.call-update
  10.9 0.1 convert_reduce_fusion
  10.9 1.6 %copy.20 = bf16[128,3584]{0,1:T(8,128)(2,1)S(1)} copy(bf16[128,3584]{1,0:T(8,128)(2,1)} %param.4) | data formatting | bytes 1835008 | tf_op args[0]
  12.5 0.2 convert.18
  12.7 0.3 fusion.9
  13.1 0.3 subtract_convert_fusion
  13.3 0.1 pad_maximum_fusion
  13.4 40.6 %all-gather.3.cloned.1.call-done = bf16[2048,512]{0,1:T(8,128)(2,1)} async-done(((bf16[128,512]{0,1:T(8,128)(2,1)}), bf16[2048,512]{0,1:T(8,128)(2,1)}) %all-gather.3.cloned.1.call-update) | async-done | bytes 2097168 | tf_op jit(solution)/shard_map/all_gather | solution.py:55
  54.0 13.3 %fusion = (f32[128,4,7]{0,2,1:T(8,128)S(1)}, f32[4,2048,128,7]{2,1,3,0:T(8,128)}) fusion(pred[128,2048]{0,1:T(8,128)(4,1)S(1)} %fusion.9, bf16[2048,4,128,1]{0,2,3,1:T(8,128)(2,1)} %bitcast.42, bf16[128,4,7,128]{0,3,2,1:T(8,128)(2,1)S(1)} %bitcast.40), kind=kOutput, calls=%fused_computation.2 | convolution fusion | flops 1901064704 | bytes 32651264 | tf_op jit(solution)/shard_map/qkgd,skd->qkgs/dot_general | solution.py:66
  67.4 13.2 %fusion.1 = f32[128,4,7]{0,2,1:T(8,128)S(1)} fusion(f32[4,2048,128,7]{2,1,3,0:T(8,128)} %get-tuple-element.14, f32[128,4,7]{0,2,1:T(8,128)S(1)} %broadcast_maximum_fusion, pred[128,2048]{0,1:T(8,128)(4,1)S(1)} %fusion.9), kind=kLoop, calls=%fused_computation.3 | loop fusion | flops 36696576 | bytes 29650944 | tf_op jit(solution)/shard_map/reduce_sum | solution.py:72
  80.6 16.2 %all-gather.5.cloned.1.call-done = bf16[2048,512]{1,0:T(8,128)(2,1)} async-done(((bf16[128,512]{1,0:T(8,128)(2,1)}), bf16[2048,512]{1,0:T(8,128)(2,1)}) %all-gather.5.cloned.1.call-update) | async-done | bytes 2097168 | tf_op jit(solution)/shard_map/all_gather | solution.py:56
  96.8 2.9 %copy.23 = bf16[2048,512]{0,1:T(8,128)(2,1)S(1)} copy(bf16[2048,512]{1,0:T(8,128)(2,1)} %all-gather.5.cloned.1.call-done) | data formatting | bytes 4194304 | tf_op jit(solution)/shard_map/all_gather | solution.py:56
  99.7 13.2 %fusion.6 = bf16[128,4,7,128]{0,3,2,1:T(8,128)(2,1)S(1)} fusion(bf16[2048,4,128,1]{0,2,3,1:T(8,128)(2,1)S(1)} %bitcast.41, f32[4,2048,128,7]{2,1,3,0:T(8,128)} %get-tuple-element.14, f32[128,4,7]{0,2,1:T(8,128)S(1)} %broadcast_maximum_fusion, pred[128,2048]{0,1:T(8,128)(4,1)S(1)} %fusion.9, f32[128,4,7]{0,2,1:T(8,128)S(1)} %fusion.1), kind=kOutput, calls=%fused_computation.8 | convolution fusion | flops 1916665856 | bytes 32665600 | tf_op jit(solution)/shard_map/qkgs,skd->qkgd/dot_general | solution.py:73
  112.9 1.3 %copy.25 = bf16[128,3584]{1,0:T(8,128)(2,1)} copy(bf16[128,3584]{0,1:T(8,128)(2,1)S(1)} %bitcast.44) | data formatting | bytes 1835008 | tf_op jit(solution)/shard_map/convert_element_type | solution.py:78
  (5 shorter events, 0.1 us)
Async XLA Ops:
  6.5 47.5 %all-gather.3.cloned.1.call-start = ((), (), s32[]{:S(2)}) async-start(), calls=%async_computation | async-start | bytes 2228224 | tf_op jit(solution)/shard_map/all_gather | solution.py:55
  10.1 86.7 %all-gather.5.cloned.1.call-start = ((), (), s32[]{:S(2)}) async-start(), calls=%async_computation.1 | async-start | bytes 2228224 | tf_op jit(solution)/shard_map/all_gather | solution.py:56
Sparse Core Ops, SparseCore 0:
  10.2 43.7 all-gather.2
  56.2 40.5 all-gather.4
where the time goes:
time: 121 us
  waiting for transfers between devices  57.5 us (48%)
  matrix products  26.5 us (22%)
  other arithmetic  16.7 us (14%)
  between operations  13.5 us (11%)
  local copies, waits for them, and re-layouts  6.76 us (6%)
    all_gather x1, waiting for transfers between devices, per_device(): k_piece = lax.all_gather(k_rot, 'seq', axis=0, tiled=True)  40.6 us
    all_gather x1, waiting for transfers between devices, per_device(): v_piece = lax.all_gather(values, 'seq', axis=0, tiled=True)  16.2 us
    dot_general x1, matrix products, per_device(): jnp.einsum('qkgd,skd->qkgs', q_heads, k_heads, preferred_element_type=jnp...  13.3 us
    reduce_sum x1, other arithmetic, per_device(): weight_sum = jnp.sum(weight, axis=-1)  13.2 us
    dot_general x1, matrix products, per_device(): jnp.einsum('qkgs,skd->qkgd', weight.astype(jnp.bfloat16), v_heads, prefer...  13.2 us
    all_gather x1, local copies, waits for them, and re-layouts, per_device(): v_piece = lax.all_gather(values, 'seq', axis=0, tiled=True)  2.93 us
  transfers between devices with their start and end apart: 2, of which 2 were waited for; matrix products, arithmetic and copies ran while one was open for 24% of the time, Pallas kernels for 0%

commit v1 on v0

v1 whole, which is shorter than its diff:
```python
import functools
import math

import jax
import jax.numpy as jnp
import numpy as np
from jax import lax
from jax.experimental import pallas as pl
from jax.experimental.pallas import tpu as pltpu
from jax.sharding import PartitionSpec as P

HEADS = 28
KV_HEADS = 4
HEAD_DIM = 128
GROUP = HEADS // KV_HEADS
HALF = HEAD_DIM // 2
ROPE_BASE = 1000000.0
NEGATIVE = -1e30
LONGEST_NUM, LONGEST_DEN = 5, 8
QUAD = 4
MESH = pl.DeviceIdType.MESH
TURN = 2.0 * math.pi
TURN_HI = float(np.float32(6.28125))
TURN_LO = float(np.float32(TURN - 6.28125))


def sine_coefficients():
    nodes = np.cos(np.pi * (np.arange(400) + 0.5) / 400) * 0.5 + 0.5
    square = nodes * (math.pi * 1.001) ** 2
    root = np.sqrt(square)
    fit = np.polynomial.Polynomial.fit(square, np.sin(root) / root, 7).convert()
    return [float(c) for c in fit.coef]


SINE = sine_coefficients()


def starts_of(position, doc_ref, docs):
    end = jnp.int32(0)
    start = jnp.zeros_like(position)
    for i in range(docs):
        end = end + doc_ref[i]
        start = jnp.where(position >= end, end, start)
    return start


def sine_cosine(angle):
    turns = jnp.floor(angle * (1.0 / TURN) + 0.5)
    rest = (angle - turns * TURN_HI) - turns * TURN_LO
    lane = lax.broadcasted_iota(jnp.int32, angle.shape, 1)
    rest = rest + jnp.where(lane < HALF, 0.0, 0.5 * math.pi)
    rest = jnp.where(rest > math.pi, rest - TURN, rest)
    square = rest * rest
    total = jnp.full_like(square, SINE[-1])
    for c in SINE[-2::-1]:
        total = total * square + c
    return total * rest


def kernel(n, doc_ref, freq_ref, q_ref, k_ref, v_ref, out_ref,
           kbuf, vbuf, cos_t, sin_t, bias, qrot, krot, peak, wsum, acc,
           send_a, send_b, send_c, recv_a, recv_b, recv_c):
    rows = q_ref.shape[0]
    docs = doc_ref.shape[0]
    levels = n // QUAD
    window = (LONGEST_NUM * n * rows // LONGEST_DEN - 1 + rows - 1) // rows
    lags = kbuf.shape[0]
    span = QUAD * rows
    me = lax.axis_index("seq")
    z, q = me // QUAD, me % QUAD
    y, core = q // 2, q % 2
    q1 = y * 2 + (1 - core)
    q2 = (1 - y) * 2 + core
    q3 = (1 - y) * 2 + (1 - core)
    up, down, across, twin = me + QUAD, me - QUAD, z * QUAD + q2, z * QUAD + q1

    def need(b, d):
        return (b < d) & (d <= b + window)

    def have_a(lag):
        return (z >= lag) & ((z - lag) * QUAD + q + window >= z * QUAD)

    def give_a(lag):
        return (z + 1 < levels) & ((z - lag) * QUAD + q + window >= (z + 1) * QUAD) & (z >= lag)

    def moves_b(lag, source, target, beside):
        b, base = (z - lag) * QUAD + source, z * QUAD
        return (z >= lag) & (need(b, base + target) | need(b, base + beside))

    def moves_c(lag, source, target):
        return (z >= lag) & need((z - lag) * QUAD + source, z * QUAD + target)

    def copy_of(part, source, lag, slot, send, recv, where):
        buf = (kbuf, vbuf)[part]
        return pltpu.make_async_remote_copy(
            src_ref=source, dst_ref=buf.at[lag, slot], send_sem=send, recv_sem=recv,
            device_id={"seq": where}, device_id_type=MESH)

    def held(part, lag, slot):
        if lag == 0 and slot is q:
            return (k_ref, v_ref)[part]
        return (kbuf, vbuf)[part].at[lag, slot]

    def copy_a(part, lag):
        return copy_of(part, held(part, lag, q), lag + 1, q, send_a.at[lag, part], recv_a.at[lag + 1, part], up)

    def copy_b(part, lag):
        return copy_of(part, held(part, lag, q), lag, q, send_b.at[lag, part], recv_b.at[lag, part], across)

    def copy_c(part, lag, which):
        slot = (q, q2)[which]
        return copy_of(part, held(part, lag, slot), lag, slot, send_c.at[lag, which, part],
                       recv_c.at[lag, which, part], twin)

    def arrival(part, lag, slot, recv, sender):
        return copy_of(part, (kbuf, vbuf)[part].at[lag, slot], lag, slot, send_a.at[0, part], recv, sender)

    barrier = pltpu.get_barrier_semaphore()
    pl.semaphore_signal(barrier, inc=1, device_id={"seq": twin}, device_id_type=MESH)
    pl.semaphore_signal(barrier, inc=1, device_id={"seq": across}, device_id_type=MESH)

    @pl.when(z + 1 < levels)
    def _():
        pl.semaphore_signal(barrier, inc=1, device_id={"seq": up}, device_id_type=MESH)

    @pl.when(z > 0)
    def _():
        pl.semaphore_signal(barrier, inc=1, device_id={"seq": down}, device_id_type=MESH)

    pl.semaphore_wait(barrier, 2 + jnp.where(z > 0, 1, 0) + jnp.where(z + 1 < levels, 1, 0))

    def forward_a(lag):
        for part in range(2):
            if lag > 0:
                @pl.when(have_a(lag))
                def _(part=part):
                    arrival(part, lag, q, recv_a.at[lag, part], down).wait_recv()

            if lag + 1 < lags:
                @pl.when(give_a(lag))
                def _(part=part):
                    copy_a(part, lag).start()

            @pl.when(moves_b(lag, q, q2, q3))
            def _(part=part):
                copy_b(part, lag).start()

            @pl.when(moves_c(lag, q, q1))
            def _(part=part):
                copy_c(part, lag, 0).start()

    def forward_b(lag):
        for part in range(2):
            @pl.when(moves_b(lag, q2, q, q1))
            def _(part=part):
                arrival(part, lag, q2, recv_b.at[lag, part], across).wait_recv()

            @pl.when(moves_c(lag, q2, q1))
            def _(part=part):
                copy_c(part, lag, 1).start()

    def land_c(lag):
        for part in range(2):
            @pl.when(moves_c(lag, q1, q))
            def _(part=part):
                arrival(part, lag, q1, recv_c.at[lag, 0, part], twin).wait_recv()

            @pl.when(moves_c(lag, q3, q))
            def _(part=part):
                arrival(part, lag, q3, recv_c.at[lag, 1, part], twin).wait_recv()

    forward_a(0)

    freq = freq_ref[:1, :]
    row_pos = me * rows + lax.broadcasted_iota(jnp.int32, (rows, rows), 1)
    row_start = starts_of(row_pos, doc_ref, docs)
    lane = lax.broadcasted_iota(jnp.int32, (rows, HEAD_DIM), 1)

    def tables(lag, slot):
        first = ((z - lag) * QUAD + slot) * rows
        at = first + lax.broadcasted_iota(jnp.int32, (rows, HEAD_DIM), 0)
        within = (at - starts_of(at, doc_ref, docs)).astype(jnp.float32)
        both = sine_cosine(within * freq)
        turned = pltpu.roll(both, HALF, 1)
        cos_t[lag, slot] = jnp.where(lane < HALF, turned, both)
        sin_t[lag, slot] = jnp.where(lane < HALF, -both, turned)
        s = first + lax.broadcasted_iota(jnp.int32, (rows, rows), 0)
        allowed = (s <= row_pos) & (s >= row_start)
        bias[lag, slot] = jnp.where(allowed, 0.0, NEGATIVE)

    def rotated(x, lag, slot):
        x = x.astype(jnp.float32)
        return (x * cos_t[lag, slot] + pltpu.roll(x, HALF, 1) * sin_t[lag, slot]).astype(jnp.bfloat16)

    def low_slot(lag):
        return max(0, lag * QUAD - window)

    for lag in range(lags):
        @pl.when(z >= lag)
        def _(lag=lag):
            def one(slot, carry):
                tables(lag, slot)
                return carry

            lax.fori_loop(low_slot(lag), QUAD, one, 0)

            for slot, gets in ((q1, moves_c(lag, q1, q)), (q2, moves_b(lag, q2, q, q1)),
                               (q3, moves_c(lag, q3, q))) + (((q, have_a(lag)),) if lag else ()):
                @pl.when(jnp.logical_not(gets))
                def _(slot=slot):
                    kbuf[lag, slot] = jnp.zeros(kbuf.shape[2:], kbuf.dtype)
                    vbuf[lag, slot] = jnp.zeros(vbuf.shape[2:], vbuf.dtype)

    kbuf[0, q] = k_ref[...]
    vbuf[0, q] = v_ref[...]

    def turn_queries(h, carry):
        cols = pl.ds(pl.multiple_of(h * HEAD_DIM, HEAD_DIM), HEAD_DIM)
        qrot[h // GROUP, pl.ds(pl.multiple_of((h % GROUP) * rows, rows), rows), :] = rotated(q_ref[:, cols], 0, q)
        return carry

    lax.fori_loop(0, HEADS, turn_queries, 0)

    scale = HEAD_DIM ** -0.5 * math.log2(math.e)

    def attend(lag):
        low = low_slot(lag)
        keys = (QUAD - low) * rows

        def one(kv, carry):
            cols = pl.ds(pl.multiple_of(kv * HEAD_DIM, HEAD_DIM), HEAD_DIM)
            for slot in range(low, QUAD):
                krot[pl.ds((slot - low) * rows, rows), :] = rotated(kbuf[lag, slot, :, cols], lag, slot)
            scores = lax.dot_general(krot[pl.ds(0, keys), :], qrot[kv], (((1,), (1,)), ((), ())),
                                     preferred_element_type=jnp.float32)
            mask = bias[lag, low:].reshape(keys, rows)
            scores = scores + jnp.concatenate([mask] * GROUP, axis=1)
            top = jnp.max(scores, axis=0, keepdims=True)
            if lag > 0:
                old = peak[kv][:1]
                top = jnp.maximum(top, old)
            weight = jnp.exp2((scores - top) * scale)
            sums = jnp.sum(weight, axis=0, keepdims=True)
            vals = vbuf[lag, low:, :, cols].reshape(keys, HEAD_DIM)
            part = lax.dot_general(vals, weight.astype(jnp.bfloat16), (((0,), (0,)), ((), ())),
                                   preferred_element_type=jnp.float32)
            if lag > 0:
                shrink = jnp.exp2((old - top) * scale)
                sums = wsum[kv][:1] * shrink + sums
                part = acc[kv] * shrink + part
            peak[kv] = jnp.broadcast_to(top, peak.shape[1:])
            wsum[kv] = jnp.broadcast_to(sums, wsum.shape[1:])
            acc[kv] = part
            return carry

        lax.fori_loop(0, KV_HEADS, one, 0)

    for lag in range(lags + 1):
        if lag + 1 < lags:
            forward_a(lag + 1)
        if lag < lags:
            forward_b(lag)
            land_c(lag)

            if lag == 0:
                attend(0)
            else:
                @pl.when(z >= lag)
                def _(lag=lag):
                    attend(lag)

    def finish(kv, carry):
        result = acc[kv] / wsum[kv][:1]
        for g in range(GROUP):
            cols = pl.ds(pl.multiple_of((kv * GROUP + g) * HEAD_DIM, HEAD_DIM), HEAD_DIM)
            out_ref[:, cols] = result[:, g * rows:(g + 1) * rows].T.astype(out_ref.dtype)
        return carry

    lax.fori_loop(0, KV_HEADS, finish, 0)

    for lag in range(lags):
        for part in range(2):
            if lag + 1 < lags:
                @pl.when(give_a(lag))
                def _(lag=lag, part=part):
                    copy_a(part, lag).wait_send()

            @pl.when(moves_b(lag, q, q2, q3))
            def _(lag=lag, part=part):
                copy_b(part, lag).wait_send()

            @pl.when(moves_c(lag, q, q1))
            def _(lag=lag, part=part):
                copy_c(part, lag, 0).wait_send()

            @pl.when(moves_c(lag, q2, q1))
            def _(lag=lag, part=part):
                copy_c(part, lag, 1).wait_send()


def per_device(n, queries, keys, values, doc_lengths):
    rows, width = queries.shape
    kv_width = keys.shape[1]
    window = (LONGEST_NUM * n * rows // LONGEST_DEN - 1 + rows - 1) // rows
    lags = min(n // QUAD, (window + QUAD - 1) // QUAD + 1)
    freq = ROPE_BASE ** (-2.0 * (np.arange(HEAD_DIM) % HALF) / HEAD_DIM)
    freq = jnp.asarray(np.tile(freq.astype(np.float32)[None, :], (8, 1)))
    vmem = pl.BlockSpec(memory_space=pltpu.VMEM)
    dma = pltpu.SemaphoreType.DMA
    return pl.pallas_call(
        functools.partial(kernel, n),
        out_shape=jax.ShapeDtypeStruct((rows, width), jnp.bfloat16),
        in_specs=[pl.BlockSpec(memory_space=pltpu.SMEM), vmem, vmem, vmem, vmem],
        out_specs=vmem,
        scratch_shapes=[
            pltpu.VMEM((lags, QUAD, rows, kv_width), jnp.bfloat16),
            pltpu.VMEM((lags, QUAD, rows, kv_width), jnp.bfloat16),
            pltpu.VMEM((lags, QUAD, rows, HEAD_DIM), jnp.float32),
            pltpu.VMEM((lags, QUAD, rows, HEAD_DIM), jnp.float32),
            pltpu.VMEM((lags, QUAD, rows, rows), jnp.float32),
            pltpu.VMEM((KV_HEADS, GROUP * rows, HEAD_DIM), jnp.bfloat16),
            pltpu.VMEM((QUAD * rows, HEAD_DIM), jnp.bfloat16),
            pltpu.VMEM((KV_HEADS, 8, GROUP * rows), jnp.float32),
            pltpu.VMEM((KV_HEADS, 8, GROUP * rows), jnp.float32),
            pltpu.VMEM((KV_HEADS, HEAD_DIM, GROUP * rows), jnp.float32),
            dma((lags, 2)), dma((lags, 2)), dma((lags, 2, 2)),
            dma((lags, 2)), dma((lags, 2)), dma((lags, 2, 2)),
        ],
        compiler_params=pltpu.CompilerParams(
            collective_id=0, has_side_effects=True, vmem_limit_bytes=60 * 1024 * 1024
        ),
    )(doc_lengths, freq, queries, keys, values)


def solution(mesh):
    return jax.shard_map(
        functools.partial(per_device, mesh.shape["seq"]),
        mesh=mesh,
        in_specs=(
            P(("grp", "seq"), None),
            P(("grp", "seq"), None),
            P(("grp", "seq"), None),
            P("grp"),
        ),
        out_specs=P(("grp", "seq"), None),
        check_vma=False,
    )
```

time: 121 us -> 36.5 us (0.30)
  the two profiles are of different devices: /device:TPU:0 before, /device:TPU:26 now
where the time goes in v1:
time: 36.5 us; the launch traced here: 36.3 us
  Pallas kernels  34.1 us (93%)
  local copies, waits for them, and re-layouts  2.16 us (6%)
    pallas_call x1, Pallas kernels, per_device(): pl.pallas_call(functools.partial(kernel, n), out_shape=jax.ShapeDtypeStru...  34.1 us
    unnamed x1, local copies, waits for them, and re-layouts  2.16 us

profile of v1, /device:TPU:26, one launch (start us, length us, event | category | flops | bytes accessed | tf_op | source)
XLA Modules:
  0.0 36.3 jit_solution(13728816281177708512)
XLA Ops:
  0.0 34.1 %shard_map.55 = bf16[128,3584]{1,0:T(8,128)(2,1)} custom-call(s32[8]{0:T(128)} %doc_ref.1, f32[8,128]{1,0:T(8,128)} %constant.2.clone.freq_ref, bf16[128,3584]{1,0:T(8,128)(2,1)} %q_ref.1, bf16[128,512]{1,0:T(8,128)(2,1)} %k_ref.1, bf16[128,512]{1,0:T(8,128)(2,1)} %v_ref.1), custom_call_target="tpu_custom_call" | custom-call | tf_op jit(solution)/shard_map/pallas_call | solution.py:310
  34.1 2.2 %copy.7 = bf16[128,3584]{1,0:T(8,128)(2,1)} copy(bf16[128,3584]{1,0:T(8,128)(2,1)} %shard_map.55) | data formatting | bytes 1835008

commit v2 on v1

--- a/solution.py
+++ b/solution.py
@@ -18,6 +18,8 @@
 NEGATIVE = -1e30
 LONGEST_NUM, LONGEST_DEN = 5, 8
 QUAD = 4
+CHUNKS = 2
+PARTS = 2 * CHUNKS
 MESH = pl.DeviceIdType.MESH
 TURN = 2.0 * math.pi
 TURN_HI = float(np.float32(6.28125))
@@ -59,12 +61,16 @@
 
 def kernel(n, doc_ref, freq_ref, q_ref, k_ref, v_ref, out_ref,
            kbuf, vbuf, cos_t, sin_t, bias, qrot, krot, peak, wsum, acc,
-           send_a, send_b, send_c, recv_a, recv_b, recv_c):
+           send_a, send_b, send_c, send_far, recv_a, recv_b, recv_c):
     rows = q_ref.shape[0]
     docs = doc_ref.shape[0]
     levels = n // QUAD
     window = (LONGEST_NUM * n * rows // LONGEST_DEN - 1 + rows - 1) // rows
     lags = kbuf.shape[0]
+    direct = False
+    far = lags - 1
+    relay_lags = lags - 1 if direct else lags
+    wide = k_ref.shape[1] // CHUNKS
     span = QUAD * rows
     me = lax.axis_index("seq")
     z, q = me // QUAD, me % QUAD
@@ -90,16 +96,19 @@
     def moves_c(lag, source, target):
         return (z >= lag) & need((z - lag) * QUAD + source, z * QUAD + target)
 
+    def place(part, lag, slot):
+        cols = pl.ds(part // 2 * wide, wide)
+        return (kbuf, vbuf)[part % 2].at[lag, slot, :, cols]
+
     def copy_of(part, source, lag, slot, send, recv, where):
-        buf = (kbuf, vbuf)[part]
         return pltpu.make_async_remote_copy(
-            src_ref=source, dst_ref=buf.at[lag, slot], send_sem=send, recv_sem=recv,
+            src_ref=source, dst_ref=place(part, lag, slot), send_sem=send, recv_sem=recv,
             device_id={"seq": where}, device_id_type=MESH)
 
     def held(part, lag, slot):
         if lag == 0 and slot is q:
-            return (k_ref, v_ref)[part]
-        return (kbuf, vbuf)[part].at[lag, slot]
+            return (k_ref, v_ref)[part % 2].at[:, pl.ds(part // 2 * wide, wide)]
+        return place(part, lag, slot)
 
     def copy_a(part, lag):
         return copy_of(part, held(part, lag, q), lag + 1, q, send_a.at[lag, part], recv_a.at[lag + 1, part], up)
@@ -112,8 +121,16 @@
         return copy_of(part, held(part, lag, slot), lag, slot, send_c.at[lag, which, part],
                        recv_c.at[lag, which, part], twin)
 
+    gives_far = (q >= 2) & (z + far < levels) & (
+        need(me, me + far * QUAD - 2) | need(me, (z + far) * QUAD + q3))
+    takes_far = (q < 2) & moves_b(far, q2, q, q1)
+
+    def copy_far(part):
+        return copy_of(part, held(part, 0, q), far, q, send_far.at[part], recv_b.at[far, part],
+                       (z + far) * QUAD + q2)
+
     def arrival(part, lag, slot, recv, sender):
-        return copy_of(part, (kbuf, vbuf)[part].at[lag, slot], lag, slot, send_a.at[0, part], recv, sender)
+        return copy_of(part, place(part, lag, slot), lag, slot, send_a.at[0, part], recv, sender)
 
     barrier = pltpu.get_barrier_semaphore()
     pl.semaphore_signal(barrier, inc=1, device_id={"seq": twin}, device_id_type=MESH)
@@ -127,16 +144,28 @@
     def _():
         pl.semaphore_signal(barrier, inc=1, device_id={"seq": down}, device_id_type=MESH)
 
-    pl.semaphore_wait(barrier, 2 + jnp.where(z > 0, 1, 0) + jnp.where(z + 1 < levels, 1, 0))
-
-    def forward_a(lag):
-        for part in range(2):
+    extra = 0
+    if direct:
+        @pl.when(gives_far)
+        def _():
+            pl.semaphore_signal(barrier, inc=1, device_id={"seq": (z + far) * QUAD + q2}, device_id_type=MESH)
+
+        @pl.when(takes_far)
+        def _():
+            pl.semaphore_signal(barrier, inc=1, device_id={"seq": (z - far) * QUAD + q2}, device_id_type=MESH)
+
+        extra = jnp.where(gives_far, 1, 0) + jnp.where(takes_far, 1, 0)
+
+    pl.semaphore_wait(barrier, 2 + extra + jnp.where(z > 0, 1, 0) + jnp.where(z + 1 < levels, 1, 0))
+
+    def forward_a(lag, chunk):
+        for part in (2 * chunk, 2 * chunk + 1):
             if lag > 0:
                 @pl.when(have_a(lag))
                 def _(part=part):
                     arrival(part, lag, q, recv_a.at[lag, part], down).wait_recv()
 
-            if lag + 1 < lags:
+            if lag + 1 < relay_lags:
                 @pl.when(give_a(lag))
                 def _(part=part):
                     copy_a(part, lag).start()
@@ -149,9 +178,12 @@
             def _(part=part):
                 copy_c(part, lag, 0).start()
 
-    def forward_b(lag):
-        for part in range(2):
-            @pl.when(moves_b(lag, q2, q, q1))
+    def gets_b(lag):
+        return takes_far if direct and lag == far else moves_b(lag, q2, q, q1)
+
+    def forward_b(lag, chunk):
+        for part in (2 * chunk, 2 * chunk + 1):
+            @pl.when(gets_b(lag))
             def _(part=part):
                 arrival(part, lag, q2, recv_b.at[lag, part], across).wait_recv()
 
@@ -159,17 +191,24 @@
             def _(part=part):
                 copy_c(part, lag, 1).start()
 
-    def land_c(lag):
-        for part in range(2):
-            @pl.when(moves_c(lag, q1, q))
-            def _(part=part):
-                arrival(part, lag, q1, recv_c.at[lag, 0, part], twin).wait_recv()
+    def land_c(lag, chunk):
+        for part in (2 * chunk, 2 * chunk + 1):
+            if not (direct and lag == far):
+                @pl.when(moves_c(lag, q1, q))
+                def _(part=part):
+                    arrival(part, lag, q1, recv_c.at[lag, 0, part], twin).wait_recv()
 
             @pl.when(moves_c(lag, q3, q))
             def _(part=part):
                 arrival(part, lag, q3, recv_c.at[lag, 1, part], twin).wait_recv()
 
-    forward_a(0)
+    for chunk in range(CHUNKS):
+        forward_a(0, chunk)
+    if direct:
+        @pl.when(gives_far)
+        def _():
+            for part in range(PARTS):
+                copy_far(part).start()
 
     freq = freq_ref[:1, :]
     row_pos = me * rows + lax.broadcasted_iota(jnp.int32, (rows, rows), 1)
@@ -223,7 +262,7 @@
 
     scale = HEAD_DIM ** -0.5 * math.log2(math.e)
 
-    def attend(lag):
+    def attend(lag, chunk):
         low = low_slot(lag)
         keys = (QUAD - low) * rows
 
@@ -253,21 +292,21 @@
             acc[kv] = part
             return carry
 
-        lax.fori_loop(0, KV_HEADS, one, 0)
-
-    for lag in range(lags + 1):
-        if lag + 1 < lags:
-            forward_a(lag + 1)
-        if lag < lags:
-            forward_b(lag)
-            land_c(lag)
-
-            if lag == 0:
-                attend(0)
-            else:
-                @pl.when(z >= lag)
-                def _(lag=lag):
-                    attend(lag)
+        lax.fori_loop(chunk * KV_HEADS // CHUNKS, (chunk + 1) * KV_HEADS // CHUNKS, one, 0, unroll=True)
+
+    order = list(range(lags))
+    if direct:
+        order = order[:-2] + [far, far - 1]
+    for step, lag in enumerate(order):
+        for chunk in range(CHUNKS):
+            if step + 1 < relay_lags:
+                forward_a(step + 1, chunk)
+            forward_b(lag, chunk)
+            land_c(lag, chunk)
+
+            @pl.when((z >= lag) & ((z - lag) * QUAD + QUAD - 1 + window >= me))
+            def _(lag=lag, chunk=chunk):
+                attend(lag, chunk)
 
     def finish(kv, carry):
         result = acc[kv] / wsum[kv][:1]
@@ -278,20 +317,26 @@
 
     lax.fori_loop(0, KV_HEADS, finish, 0)
 
-    for lag in range(lags):
-        for part in range(2):
-            if lag + 1 < lags:
+    for part in range(PARTS):
+        if direct:
+            @pl.when(gives_far)
+            def _(part=part):
+                copy_far(part).wait_send()
+
+        for lag in range(lags):
+            if lag + 1 < relay_lags:
                 @pl.when(give_a(lag))
                 def _(lag=lag, part=part):
                     copy_a(part, lag).wait_send()
 
-            @pl.when(moves_b(lag, q, q2, q3))
-            def _(lag=lag, part=part):
-                copy_b(part, lag).wait_send()
-
-            @pl.when(moves_c(lag, q, q1))
-            def _(lag=lag, part=part):
-                copy_c(part, lag, 0).wait_send()
+            if lag < relay_lags:
+                @pl.when(moves_b(lag, q, q2, q3))
+                def _(lag=lag, part=part):
+                    copy_b(part, lag).wait_send()
+
+                @pl.when(moves_c(lag, q, q1))
+                def _(lag=lag, part=part):
+                    copy_c(part, lag, 0).wait_send()
 
             @pl.when(moves_c(lag, q2, q1))
             def _(lag=lag, part=part):
@@ -323,8 +368,8 @@
             pltpu.VMEM((KV_HEADS, 8, GROUP * rows), jnp.float32),
             pltpu.VMEM((KV_HEADS, 8, GROUP * rows), jnp.float32),
             pltpu.VMEM((KV_HEADS, HEAD_DIM, GROUP * rows), jnp.float32),
-            dma((lags, 2)), dma((lags, 2)), dma((lags, 2, 2)),
-            dma((lags, 2)), dma((lags, 2)), dma((lags, 2, 2)),
+            dma((lags, PARTS)), dma((lags, PARTS)), dma((lags, 2, PARTS)), dma((PARTS,)),
+            dma((lags, PARTS)), dma((lags, PARTS)), dma((lags, 2, PARTS)),
         ],
         compiler_params=pltpu.CompilerParams(
             collective_id=0, has_side_effects=True, vmem_limit_bytes=60 * 1024 * 1024

time: 36.5 us -> 34.2 us (0.937)
  Pallas kernels: 34.1 us -> 31.9 us
    pallas_call x1, Pallas kernels: 34.1 us -> 31.9 us  [per_device(): pl.pallas_call(functools.partial(kernel, n), out_shape=jax.ShapeDtypeStru...]
where the time goes in v2:
time: 34.2 us; the launch traced here: 34 us
  Pallas kernels  31.9 us (93%)
  local copies, waits for them, and re-layouts  2.16 us (6%)
    pallas_call x1, Pallas kernels, per_device(): pl.pallas_call(functools.partial(kernel, n), out_shape=jax.ShapeDtypeStru...  31.9 us
    unnamed x1, local copies, waits for them, and re-layouts  2.16 us

profile of v2, /device:TPU:26, one launch (start us, length us, event | category | flops | bytes accessed | tf_op | source)
XLA Modules:
  0.0 34.0 jit_solution(8506082069154243253)
XLA Ops:
  0.0 31.9 %shard_map.55 = bf16[128,3584]{1,0:T(8,128)(2,1)} custom-call(s32[8]{0:T(128)} %doc_ref.1, f32[8,128]{1,0:T(8,128)} %constant.2.clone.freq_ref, bf16[128,3584]{1,0:T(8,128)(2,1)} %q_ref.1, bf16[128,512]{1,0:T(8,128)(2,1)} %k_ref.1, bf16[128,512]{1,0:T(8,128)(2,1)} %v_ref.1), custom_call_target="tpu_custom_call" | custom-call | tf_op jit(solution)/shard_map/pallas_call | solution.py:355
  31.9 2.2 %copy.7 = bf16[128,3584]{1,0:T(8,128)(2,1)} copy(bf16[128,3584]{1,0:T(8,128)(2,1)} %shard_map.55) | data formatting | bytes 1835008
